TPU v7x, 512 devices: a whole 4x8x8 slice. The times are simulated.
512 devices in a mesh: dp: 4 (over x), expert: 32 (over z, y_hi, core), mp: 4 (over y_lo).
Axes of the slice: x: 4, y: 8 (y_hi: 2, y_lo: 4; y = y_hi * 4 + y_lo), z: 8, core: 2. Of those that a mesh axis runs over, the one named last changes fastest.
Arguments:
- tokens: bfloat16 [16384, 2048], P(('dp', 'expert'), 'mp'), parts along dimension 0, may hold values from -6 to 6
- routes: int32 [16384, 2], P(('dp', 'expert')), parts along dimension 0, may hold values from 0 to 7, all different within a row; in each aligned block of 128 rows (0 to 127, 128 to 255, ...) at most 48 rows name the same one
- gate_num: int32 [16384], P(('dp', 'expert')), parts along dimension 0, may hold values from 1 to 63
- capacity: int32 [8], replicated, may hold values from 24 to 48
- w_up: bfloat16 [2048, 57344], P(None, ('expert', 'mp')), may hold values from -0.125 to 0.125
- w_down: bfloat16 [57344, 2048], P(('expert', 'mp')), may hold values from -0.0625 to 0.0625
Outputs:
- mixed: bfloat16 [16384, 2048], P(('dp', 'expert'), 'mp'), parts along dimension 0
There are 4 independent parts, one for each index of `dp`. A program takes and returns all parts, laid end to end along the dimension named above; an argument that names none is the same for every part. Nothing has to cross between parts.
Inputs may be any that keep to these rules, and one draw needn't show every extreme that they name: `routes`: each row names two different experts; in each aligned block of 128 rows no expert is named by more than 48 rows, a bound that some block reaches.
All inputs are finite; a program needn't handle non-finite values.
Results may differ from a plain program's by a relative error of at most 0.0085.
Values may be sent and summed in bfloat16 or wider, within the bound.
No kernel may reach another device: no remote copies, remote signals or barrier semaphores. Data moves between devices by JAX's collectives and lax.ppermute only.
A program may use at most 64 MiB of HBM per device.

v0:
```python
import jax
import jax.numpy as jnp
from jax import lax
from jax.sharding import PartitionSpec as P


def split_up(shard, dim, length):
    before, after = (shard.shape[:dim], shard.shape[dim + 1 :])
    return jnp.moveaxis(shard.reshape(*before, length, -1, *after), dim, 0)


def edges_of(length, count):
    step = length // count
    if step >= 8:
        step -= step % 8
    return [step * k for k in range(1, count)]


def laid_out(tiles, dim):
    lengths = list(tiles.shape[1:])
    lengths[dim] *= tiles.shape[0]
    return jnp.moveaxis(tiles, 0, dim).reshape(lengths)


def cut_exchange(shard, axis, pieces, split_dim, concat_dim):
    tiles = split_up(shard, split_dim, lax.axis_size(axis))
    widest = max(range(1, max(2, tiles.ndim - 1)), key=lambda d: tiles.shape[d])
    finished = []
    for section in jnp.split(tiles, edges_of(tiles.shape[widest], pieces), axis=widest):
        if section.size:
            finished.append(lax.all_to_all(section, axis, split_axis=0, concat_axis=0, tiled=True))
    return laid_out(jnp.concatenate(finished, axis=widest), concat_dim)


def copy_for_each(shard, axis):
    copies = jnp.broadcast_to(shard, (lax.axis_size(axis), *shard.shape))
    return lax.all_to_all(copies, axis, split_axis=0, concat_axis=0, tiled=True)


def gather_directly(shard, axis, dim):
    tiles = copy_for_each(shard, axis)
    return laid_out(tiles, dim)


def sent_and_summed(shard, axis, dim):
    length = lax.axis_size(axis)
    tiles = lax.all_to_all(split_up(shard, dim, length), axis, 0, 0, tiled=True)
    return jnp.sum(tiles.astype(jnp.float32), axis=0)


def per_device(tokens, routes, gate_num, capacity, w_up, w_down):
    token_count = routes.shape[0]
    expert_count = capacity.shape[0]
    group_size = lax.axis_size("expert") // expert_count
    slot_count = min(token_count, 3 * token_count // expert_count)
    feature_width = w_up.shape[0]
    expert_ids = jnp.arange(expert_count, dtype=jnp.int32)
    matches = routes[:, :, None] == expert_ids[None, None, :]
    named_count = matches.sum(axis=1).astype(jnp.float32)
    token_ids = jnp.arange(token_count, dtype=jnp.int32)
    lower_mask = (token_ids[:, None] > token_ids[None, :]).astype(jnp.float32)
    positions = jnp.dot(
        lower_mask, named_count, precision=lax.Precision.HIGHEST, preferred_element_type=jnp.float32
    ).astype(jnp.int32)
    route_pos = jnp.sum(jnp.where(matches, positions[:, None, :], 0), axis=2)
    route_cap = jnp.sum(jnp.where(matches, capacity[None, None, :], 0), axis=2)
    kept_mask = route_pos < route_cap
    slot_index = jnp.where(kept_mask, routes * slot_count + route_pos, -1)
    first_share = gate_num.astype(jnp.float32) / 64.0
    weights = jnp.where(kept_mask, jnp.stack([first_share, 1.0 - first_share], axis=1), 0.0)
    slot_ids = jnp.arange(expert_count * slot_count, dtype=jnp.int32)
    dispatch_matrix = jnp.any(slot_ids[:, None, None] == slot_index[None, :, :], axis=2).astype(
        jnp.bfloat16
    )
    combine_hits = slot_ids[None, :, None] == slot_index[:, None, :]
    combine_matrix = jnp.sum(jnp.where(combine_hits, weights[:, None, :], 0.0), axis=2)
    whole = gather_directly(tokens, "mp", 1)
    buffer = jnp.dot(dispatch_matrix, whole, preferred_element_type=jnp.float32).astype(
        jnp.bfloat16
    )
    width = buffer.shape[1]
    grouped = buffer.reshape(expert_count, 1, slot_count, width)
    copies = jnp.broadcast_to(grouped, (expert_count, group_size, slot_count, width))
    received = lax.all_to_all(
        copies.reshape(expert_count * group_size, slot_count, width),
        "expert",
        split_axis=0,
        concat_axis=0,
        tiled=True,
    )
    source_count, count_here, width = received.shape
    flat_rows = received.reshape(source_count * count_here, width)
    hidden = jax.nn.silu(jnp.dot(flat_rows, w_up, preferred_element_type=jnp.float32)).astype(
        jnp.bfloat16
    )
    partial_value = jnp.dot(hidden, w_down, preferred_element_type=jnp.float32).astype(jnp.bfloat16)
    answered = cut_exchange(
        partial_value.reshape(source_count, count_here, width), "expert", 2, 0, 0
    )
    summed = (
        answered.astype(jnp.float32)
        .reshape(expert_count, group_size, slot_count, feature_width)
        .sum(axis=1)
    )
    summed = summed.reshape(expert_count * slot_count, feature_width)
    mixed = jnp.dot(
        combine_matrix, summed, precision=lax.Precision.HIGHEST, preferred_element_type=jnp.float32
    )
    return sent_and_summed(mixed.astype(jnp.bfloat16), "mp", 1).astype(jnp.bfloat16)


def solution(mesh):
    return jax.shard_map(
        per_device,
        mesh=mesh,
        in_specs=(
            P(("dp", "expert"), "mp"),
            P(("dp", "expert"), None),
            P(("dp", "expert")),
            P(),
            P(None, ("expert", "mp")),
            P(("expert", "mp"), None),
        ),
        out_specs=P(("dp", "expert"), "mp"),
        check_vma=False,
    )
```

profile of v0, /device:TPU:248, one launch (start us, length us, event | category | flops | bytes accessed | tf_op | source)
XLA Modules:
  0.0 418.0 jit_solution(8244440295219865810)
XLA Ops:
  0.0 0.0 copy-start
  0.0 1.2 copy.27
  1.2 0.9 broadcast_in_dim.70
  2.0 6.4 %all-to-all-start = ((bf16[4,128,512]{1,2,0:T(8,128)(2,1)}), bf16[4,128,512]{1,2,0:T(8,128)(2,1)S(1)}, u32[]{:S(2)}, u32[]{:S(2)}) async-start(bf16[4,128,512]{1,2,0:T(8,128)(2,1)} %broadcast_in_dim.70), calls=%async_computation | async-start | bytes 1048576 | tf_op jit(solution)/shard_map/all_to_all | solution.py:37
  8.4 0.7 convert_reduce_fusion.1
  9.1 0.1 convolution_convert_fusion.3
  9.2 0.8 select_reduce_fusion.1
  10.0 0.7 add_select_fusion
  10.8 10.0 %all-to-all-done = bf16[4,128,512]{1,2,0:T(8,128)(2,1)S(1)} async-done(((bf16[4,128,512]{1,2,0:T(8,128)(2,1)}), bf16[4,128,512]{1,2,0:T(8,128)(2,1)S(1)}, u32[]{:S(2)}, u32[]{:S(2)}) %all-to-all-start) | async-done | bytes 524320 | tf_op jit(solution)/shard_map/all_to_all | solution.py:37
  20.8 0.6 convolution_convert_fusion.1
  21.4 0.8 broadcast_in_dim.72
  22.2 154.9 %all_to_all.25 = bf16[32,48,2048]{2,1,0:T(8,128)(2,1)} all-to-all(bf16[32,48,2048]{2,1,0:T(8,128)(2,1)S(1)} %bitcast.34), channel_id=1, replica_groups=mesh['dp'=4,'expert'=32,'mp'=4] {'expert'}, dimensions={0} | all-to-all | bytes 12582912 | tf_op jit(solution)/shard_map/all_to_all | solution.py:84
  177.1 0.0 copy-done
  177.1 12.8 %convolution_convert_fusion = bf16[1536,2048]{1,0:T(8,128)(2,1)} fusion(bf16[448,2048]{1,0:T(8,128)(2,1)S(1)} %copy-done, bf16[1536,2048]{1,0:T(8,128)(2,1)} %bitcast.37, bf16[2048,448]{0,1:T(8,128)(2,1)} %param.10), kind=kOutput, calls=%fused_computation.1 | convolution fusion | flops 5643730944 | bytes 16252928 | tf_op jit(solution)/shard_map/dot_general | solution.py:96
  190.0 5.4 %fusion.5 = (bf16[32,1,24,2048]{3,2,1,0:T(8,128)(2,1)S(1)}, bf16[32,1,24,2048]{3,2,1,0:T(8,128)(2,1)}) fusion(bf16[32,1,48,2048]{3,2,1,0:T(8,128)(2,1)} %bitcast.36), kind=kLoop, calls=%fused_computation.25 | loop fusion | bytes 12582912 | tf_op jit(solution)/shard_map/split | solution.py:29
  195.4 84.7 %all_to_all.26 = bf16[32,1,24,2048]{3,2,1,0:T(8,128)(2,1)} all-to-all(bf16[32,1,24,2048]{3,2,1,0:T(8,128)(2,1)S(1)} %get-tuple-element.9), channel_id=1, replica_groups=mesh['dp'=4,'expert'=32,'mp'=4] {'expert'}, dimensions={0} | all-to-all | bytes 6291456 | tf_op jit(solution)/shard_map/all_to_all | solution.py:31
  280.0 0.0 copy-start.1
  280.0 12.5 %all-to-all-start.3 = ((bf16[32,1,24,2048]{3,2,1,0:T(8,128)(2,1)}), bf16[32,1,24,2048]{3,2,1,0:T(8,128)(2,1)}, u32[]{:S(2)}, u32[]{:S(2)}) async-start(bf16[32,1,24,2048]{3,2,1,0:T(8,128)(2,1)} %get-tuple-element.10), calls=%async_computation.3 | async-start | bytes 6291456 | tf_op jit(solution)/shard_map/all_to_all | solution.py:31
  292.5 0.0 copy-done.1
  292.5 0.1 select_reduce_fusion
  292.7 83.6 %all-to-all-done.3 = bf16[32,1,24,2048]{3,2,1,0:T(8,128)(2,1)} async-done(((bf16[32,1,24,2048]{3,2,1,0:T(8,128)(2,1)}), bf16[32,1,24,2048]{3,2,1,0:T(8,128)(2,1)}, u32[]{:S(2)}, u32[]{:S(2)}) %all-to-all-start.3) | async-done | bytes 3145760 | tf_op jit(solution)/shard_map/all_to_all | solution.py:31
  376.3 4.0 pad_maximum_fusion
  380.3 1.3 convert_reduce_fusion
  381.6 2.0 convolution_convert_fusion.2
  383.6 33.6 %all_to_all.27 = bf16[4,128,512]{2,1,0:T(8,128)(2,1)S(1)} all-to-all(bf16[4,128,512]{2,1,0:T(8,128)(2,1)S(1)} %bitcast.39), channel_id=1, replica_groups=mesh['dp'=4,'expert'=32,'mp'=4] {'mp'}, dimensions={0} | all-to-all | bytes 1048576 | tf_op jit(solution)/shard_map/all_to_all | solution.py:47
  417.3 0.7 reduce_sum.62
  (4 shorter events, 0.1 us)
Async XLA Ops:
  0.0 177.1 %copy-start = (bf16[448,2048]{1,0:T(8,128)(2,1)S(1)}, bf16[448,2048]{1,0:T(8,128)(2,1)}, u32[]{:S(2)}) copy-start(bf16[448,2048]{1,0:T(8,128)(2,1)} %param.11) | copy-start | bytes 5505028
  2.0 18.8 %all-to-all-start = ((bf16[4,128,512]{1,2,0:T(8,128)(2,1)}), bf16[4,128,512]{1,2,0:T(8,128)(2,1)S(1)}, u32[]{:S(2)}, u32[]{:S(2)}) async-start(bf16[4,128,512]{1,2,0:T(8,128)(2,1)} %broadcast_in_dim.70), calls=%async_computation | async-start | bytes 1048576 | tf_op jit(solution)/shard_map/all_to_all | solution.py:37
  280.0 12.5 %copy-start.1 = (s32[128]{0:T(128)S(1)}, s32[128]{0:T(128)}, u32[]{:S(2)}) copy-start(s32[128]{0:T(128)} %param.8) | copy-start | bytes 1540
  280.0 96.3 %all-to-all-start.3 = ((bf16[32,1,24,2048]{3,2,1,0:T(8,128)(2,1)}), bf16[32,1,24,2048]{3,2,1,0:T(8,128)(2,1)}, u32[]{:S(2)}, u32[]{:S(2)}) async-start(bf16[32,1,24,2048]{3,2,1,0:T(8,128)(2,1)} %get-tuple-element.10), calls=%async_computation.3 | async-start | bytes 6291456 | tf_op jit(solution)/shard_map/all_to_all | solution.py:31
where the time goes:
time: 418 us
  blocking collectives  273 us (65%)
  waiting for transfers between devices  93.7 us (22%)
  starting transfers between devices  18.8 us (4%)
  matrix products  15.5 us (4%)
  other arithmetic  8.38 us (2%)
  local copies, waits for them, and re-layouts  8.27 us (2%)
    all_to_all x1, blocking collectives, per_device(): lax.all_to_all(copies.reshape(expert_count * group_size, slot_count, widt...  155 us
    all_to_all x1, blocking collectives, cut_exchange(): lax.all_to_all(section, axis, split_axis=0, concat_axis=0, tiled=True)  84.7 us
    all_to_all x1, waiting for transfers between devices, cut_exchange(): lax.all_to_all(section, axis, split_axis=0, concat_axis=0, tiled=True)  83.6 us
    all_to_all x1, blocking collectives, sent_and_summed(): tiles = lax.all_to_all(split_up(shard, dim, length), axis, 0, 0, tiled=True)  33.6 us
    dot_general x1, matrix products, per_device(): jnp.dot(hidden, w_down, preferred_element_type=jnp.float32)  12.8 us
    all_to_all x1, starting transfers between devices, cut_exchange(): lax.all_to_all(section, axis, split_axis=0, concat_axis=0, tiled=True)  12.5 us
    all_to_all x1, waiting for transfers between devices, copy_for_each(): return lax.all_to_all(copies, axis, split_axis=0, concat_axis=0, tiled=True)  10 us
  transfers between devices with their start and end apart: 2, of which 2 were waited for; matrix products, arithmetic and copies ran while one was open for 1% of the time, Pallas kernels for 0%

commit v1 on v0

v1 whole, which is shorter than its diff:
```python
import jax
import jax.numpy as jnp
from jax import lax
from jax.experimental import pallas as pl
from jax.experimental.pallas import tpu as pltpu
from jax.sharding import Mesh, PartitionSpec as P

EXPERTS = 8


def ffn_body(x_ref, up_ref, down_ref, out_ref):
    chunks, rows, width = x_ref.shape
    acc = jnp.zeros((rows, up_ref.shape[0]), jnp.float32)
    for m in range(chunks):
        acc += lax.dot_general(
            x_ref[m],
            up_ref[:, m * width : (m + 1) * width],
            (((1,), (1,)), ((), ())),
            preferred_element_type=jnp.float32,
        )
    hidden = (acc / (1.0 + jnp.exp(-acc))).astype(jnp.bfloat16)
    for m in range(chunks):
        out_ref[m] = jnp.dot(
            hidden,
            down_ref[:, m * width : (m + 1) * width],
            preferred_element_type=jnp.float32,
        ).astype(jnp.bfloat16)


def ffn(x, up_t, down):
    groups, chunks, rows, width = x.shape
    hidden, features = up_t.shape
    block = pl.BlockSpec((None, chunks, rows, width), lambda g: (g, 0, 0, 0))
    whole = pl.BlockSpec((hidden, features), lambda g: (0, 0))
    return pl.pallas_call(
        ffn_body,
        grid=(groups,),
        in_specs=[block, whole, whole],
        out_specs=block,
        out_shape=jax.ShapeDtypeStruct(x.shape, jnp.bfloat16),
        compiler_params=pltpu.CompilerParams(dimension_semantics=("arbitrary",)),
        name="ffn",
    )(x, up_t, down)


def routing(routes, gate_num, capacity, slot_count):
    token_count = routes.shape[0]
    expert_count = capacity.shape[0]
    expert_ids = jnp.arange(expert_count, dtype=jnp.int32)
    matches = routes[:, :, None] == expert_ids[None, None, :]
    named_count = matches.sum(axis=1).astype(jnp.bfloat16)
    token_ids = jnp.arange(token_count, dtype=jnp.int32)
    lower_mask = (token_ids[:, None] > token_ids[None, :]).astype(jnp.bfloat16)
    positions = jnp.dot(
        lower_mask, named_count, preferred_element_type=jnp.float32
    ).astype(jnp.int32)
    route_pos = jnp.sum(jnp.where(matches, positions[:, None, :], 0), axis=2)
    route_cap = jnp.sum(jnp.where(matches, capacity[None, None, :], 0), axis=2)
    kept_mask = route_pos < route_cap
    slot_index = jnp.where(kept_mask, routes * slot_count + route_pos, -1)
    first_share = gate_num.astype(jnp.float32) / 64.0
    weights = jnp.where(kept_mask, jnp.stack([first_share, 1.0 - first_share], axis=1), 0.0)
    slot_ids = jnp.arange(expert_count * slot_count, dtype=jnp.int32)
    dispatch = jnp.any(slot_ids[:, None, None] == slot_index[None, :, :], axis=2)
    combine_hits = slot_ids[None, :, None] == slot_index[:, None, :]
    combine = jnp.sum(jnp.where(combine_hits, weights[:, None, :], 0.0), axis=2)
    return dispatch.astype(jnp.bfloat16), combine


def per_device(tokens, routes, gate_num, capacity, w_up, w_down):
    expert_count = capacity.shape[0]
    token_count, width = tokens.shape
    slot_count = min(token_count, 3 * token_count // expert_count)
    plane = ("yh", "core", "mp")
    chunks = lax.axis_size("mp")
    dispatch, combine = routing(routes, gate_num, capacity, slot_count)
    rows = jnp.dot(dispatch, tokens, preferred_element_type=jnp.float32).astype(jnp.bfloat16)
    sent = lax.all_to_all(
        rows.reshape(expert_count, slot_count, width), "z", 0, 0, tiled=True
    ).reshape(expert_count * slot_count, width)
    whole = lax.all_gather(sent, plane)
    groups = whole.shape[0] // chunks
    x = whole.reshape(groups, chunks, expert_count * slot_count, width)
    partial_value = ffn(x, w_up.T, w_down)
    summed = lax.psum_scatter(
        partial_value.reshape(groups * chunks, expert_count * slot_count, width), plane
    )
    back = lax.all_to_all(
        summed.reshape(expert_count, slot_count, width), "z", 0, 0, tiled=True
    ).reshape(expert_count * slot_count, width)
    mixed = jnp.dot(
        combine,
        back.astype(jnp.float32),
        precision=lax.Precision.HIGHEST,
        preferred_element_type=jnp.float32,
    )
    return mixed.astype(jnp.bfloat16)


def solution(mesh):
    sizes = dict(mesh.shape)
    group = sizes["expert"] // EXPERTS
    devices = mesh.devices.reshape(sizes["dp"], EXPERTS, group // 2, 2, sizes["mp"])
    fine = Mesh(devices, ("dp", "z", "yh", "core", "mp"))
    expert = ("z", "yh", "core")
    return jax.shard_map(
        per_device,
        mesh=fine,
        in_specs=(
            P(("dp", *expert), "mp"),
            P(("dp", *expert), None),
            P(("dp", *expert)),
            P(),
            P(None, (*expert, "mp")),
            P((*expert, "mp"), None),
        ),
        out_specs=P(("dp", *expert), "mp"),
        check_vma=False,
    )
```

time: 418 us -> 299 us (0.72)
  the two profiles are of different devices: /device:TPU:248 before, /device:TPU:1 now
where the time goes in v1:
time: 299 us; the launch traced here: 298 us
  waiting for transfers between devices  238 us (80%)
  blocking collectives  24.3 us (8%)
  between operations  13.4 us (4%)
  Pallas kernels  11.6 us (4%)
  starting transfers between devices  7.09 us (2%)
    reduce_scatter x1, waiting for transfers between devices, per_device(): lax.psum_scatter(partial_value.reshape(groups * chunks, expert_count * sl...  113 us
    all_gather x1, waiting for transfers between devices, per_device(): whole = lax.all_gather(sent, plane)  111 us
    all_to_all x1, blocking collectives, per_device(): lax.all_to_all(rows.reshape(expert_count, slot_count, width), 'z', 0, 0,...  24.3 us
    all_to_all x1, waiting for transfers between devices, per_device(): lax.all_to_all(summed.reshape(expert_count, slot_count, width), 'z', 0, 0...  15 us
    pallas_call x1, Pallas kernels, ffn(): pl.pallas_call(ffn_body, grid=(groups,), in_specs=[block, whole, whole],...  11.6 us
    all_to_all x1, starting transfers between devices, per_device(): lax.all_to_all(summed.reshape(expert_count, slot_count, width), 'z', 0, 0...  7.05 us
  transfers between devices with their start and end apart: 3, of which 3 were waited for; matrix products, arithmetic and copies ran while one was open for 0% of the time, Pallas kernels for 0%

profile of v1, /device:TPU:1, one launch (start us, length us, event | category | flops | bytes accessed | tf_op | source)
XLA Modules:
  0.0 298.5 jit_solution(8303587409936923185)
XLA Ops:
  6.5 0.0 copy-start
  6.5 0.0 all-gather.2.cloned.1.call-start
  6.5 0.7 convert_reduce_fusion
  7.3 0.1 convolution_convert_fusion.2
  7.4 0.8 select_reduce_fusion.1
  8.2 0.7 add_select_fusion
  8.9 0.0 copy-done
  8.9 0.2 convolution_convert_fusion
  9.2 24.3 %all_to_all.10 = bf16[8,48,512]{2,1,0:T(8,128)(2,1)} all-to-all(bf16[8,48,512]{2,1,0:T(8,128)(2,1)S(1)} %bitcast.19), channel_id=1, replica_groups=mesh['dp'=4,'z'=8,'yh'=2,'core'=2,'mp'=4] {'z'}, dimensions={0} | all-to-all | bytes 786432 | tf_op jit(solution)/shard_map/all_to_all | solution.py:78
  33.5 0.0 all-gather.2.cloned.1.call-update
  33.5 0.0 reduce-scatter.2.cloned.1.call-start
  33.6 110.5 %all-gather.2.cloned.1.call-done = bf16[16,384,512]{2,1,0:T(8,128)(2,1)} async-done(((bf16[1,384,512]{2,1,0:T(8,128)(2,1)}), bf16[16,384,512]{2,1,0:T(8,128)(2,1)}) %all-gather.2.cloned.1.call-update) | async-done | bytes 6291472 | tf_op jit(solution)/shard_map/all_gather | solution.py:81
  144.1 11.6 %ffn.1 = bf16[4,4,384,512]{3,2,1,0:T(8,128)(2,1)} custom-call(bf16[4,4,384,512]{3,2,1,0:T(8,128)(2,1)} %bitcast.16, bf16[448,2048]{1,0:T(8,128)(2,1)} %bitcast.17, bf16[448,2048]{1,0:T(8,128)(2,1)} %down_ref.1), custom_call_target="tpu_custom_call" | custom-call | tf_op jit(solution)/shard_map/ffn/pallas_call | solution.py:35
  155.7 0.0 copy-start.1
  155.7 0.0 reduce-scatter.2.cloned.1.call-update
  155.7 112.6 %reduce-scatter.2.cloned.1.call-done = bf16[1,384,512]{2,1,0:T(8,128)(2,1)} async-done(((bf16[16,384,512]{2,1,0:T(8,128)(2,1)}), bf16[1,384,512]{2,1,0:T(8,128)(2,1)}) %reduce-scatter.2.cloned.1.call-update) | async-done | bytes 393232 | tf_op jit(solution)/shard_map/reduce_scatter | solution.py:85
  268.3 7.0 %all-to-all-start.1 = ((bf16[8,48,512]{2,1,0:T(8,128)(2,1)}), bf16[8,48,512]{2,1,0:T(8,128)(2,1)S(1)}, u32[]{:S(2)}, u32[]{:S(2)}) async-start(bf16[8,48,512]{2,1,0:T(8,128)(2,1)} %bitcast.21), calls=%async_computation.2 | async-start | bytes 786432 | tf_op jit(solution)/shard_map/all_to_all | solution.py:88
  275.4 0.0 copy-done.1
  275.4 0.1 select_reduce_fusion
  275.6 15.0 %all-to-all-done.1 = bf16[8,48,512]{2,1,0:T(8,128)(2,1)S(1)} async-done(((bf16[8,48,512]{2,1,0:T(8,128)(2,1)}), bf16[8,48,512]{2,1,0:T(8,128)(2,1)S(1)}, u32[]{:S(2)}, u32[]{:S(2)}) %all-to-all-start.1) | async-done | bytes 393248 | tf_op jit(solution)/shard_map/all_to_all | solution.py:88
  290.6 1.0 convolution_convert_fusion.1
  (3 shorter events, 0.1 us)
Async XLA Ops:
  6.5 2.4 copy-start
  6.5 137.6 %all-gather.2.cloned.1.call-start = ((), (), s32[]{:S(2)}) async-start(), calls=%async_computation.3 | async-start | bytes 6684672 | tf_op jit(solution)/shard_map/all_gather | solution.py:81
  33.5 234.8 %reduce-scatter.2.cloned.1.call-start = ((), (), s32[]{:S(2)}) async-start(), calls=%async_computation.4 | async-start | bytes 6684672 | tf_op jit(solution)/shard_map/reduce_scatter | solution.py:85
  155.7 119.7 %copy-start.1 = (s32[128]{0:T(128)S(1)}, s32[128]{0:T(128)}, u32[]{:S(2)}) copy-start(s32[128]{0:T(128)} %param.8) | copy-start | bytes 1540
  268.3 22.3 %all-to-all-start.1 = ((bf16[8,48,512]{2,1,0:T(8,128)(2,1)}), bf16[8,48,512]{2,1,0:T(8,128)(2,1)S(1)}, u32[]{:S(2)}, u32[]{:S(2)}) async-start(bf16[8,48,512]{2,1,0:T(8,128)(2,1)} %bitcast.21), calls=%async_computation.2 | async-start | bytes 786432 | tf_op jit(solution)/shard_map/all_to_all | solution.py:88
Sparse Core Ops, SparseCore 0:
  33.7 110.3 all-gather.1
  155.8 112.4 reduce-scatter.1

commit v2 on v1

v2 whole, which is shorter than its diff:
```python
import jax
import jax.numpy as jnp
from jax import lax
from jax.experimental import pallas as pl
from jax.experimental.pallas import tpu as pltpu
from jax.sharding import Mesh, PartitionSpec as P

EXPERTS = 8
RING = ("yh", "mp")
STREAMS = 2


def ffn_body(place_ref, *refs):
    count = (len(refs) - 6) // 2
    x_refs, (up_a, up_b, down_a, down_b) = refs[:count], refs[count : count + 4]
    out_refs, (x_all, out_all) = refs[count + 4 : -2], refs[-2:]
    rows, width = x_refs[0].shape
    chunks = x_all.shape[1] // width
    place = place_ref[0]

    def spot(j):
        source = lax.rem(place + j, count)
        row = pl.multiple_of(lax.div(source, chunks) * rows, rows)
        col = pl.multiple_of(lax.rem(source, chunks) * width, width)
        return pl.ds(row, rows), pl.ds(col, width)

    for j in range(count):
        x_all[spot(j)] = x_refs[j][...]
    hidden = []
    for up in (up_a, up_b):
        acc = lax.dot_general(
            x_all[...], up[...], (((1,), (1,)), ((), ())), preferred_element_type=jnp.float32
        )
        hidden.append((acc / (1.0 + jnp.exp(-acc))).astype(jnp.bfloat16))
    for m in range(chunks):
        cols = slice(m * width, (m + 1) * width)
        total = jnp.dot(hidden[0], down_a[:, cols], preferred_element_type=jnp.float32)
        total += jnp.dot(hidden[1], down_b[:, cols], preferred_element_type=jnp.float32)
        out_all[:, cols] = total.astype(jnp.bfloat16)
    for j in range(count):
        out_refs[j][...] = out_all[spot(j)]


def ffn(place, chunks, weights, features):
    rows, width = chunks[0].shape
    count = len(chunks)
    total_rows = rows * count * width // features
    vmem = pl.BlockSpec(memory_space=pltpu.VMEM)
    return pl.pallas_call(
        ffn_body,
        in_specs=[pl.BlockSpec(memory_space=pltpu.SMEM)] + [vmem] * (count + 4),
        out_specs=[vmem] * count,
        out_shape=[jax.ShapeDtypeStruct((rows, width), jnp.bfloat16)] * count,
        scratch_shapes=[pltpu.VMEM((total_rows, features), jnp.bfloat16)] * 2,
        compiler_params=pltpu.CompilerParams(vmem_limit_bytes=20 << 20),
        name="ffn",
    )(place, *chunks, *weights)


def routing(routes, gate_num, capacity, slot_count):
    token_count = routes.shape[0]
    expert_count = capacity.shape[0]
    expert_ids = jnp.arange(expert_count, dtype=jnp.int32)
    matches = routes[:, :, None] == expert_ids[None, None, :]
    named_count = matches.sum(axis=1).astype(jnp.bfloat16)
    token_ids = jnp.arange(token_count, dtype=jnp.int32)
    lower_mask = (token_ids[:, None] > token_ids[None, :]).astype(jnp.bfloat16)
    positions = jnp.dot(
        lower_mask, named_count, preferred_element_type=jnp.float32
    ).astype(jnp.int32)
    route_pos = jnp.sum(jnp.where(matches, positions[:, None, :], 0), axis=2)
    route_cap = jnp.sum(jnp.where(matches, capacity[None, None, :], 0), axis=2)
    kept_mask = route_pos < route_cap
    part = slot_count // STREAMS
    stream = route_pos // part
    slot_index = (stream * expert_count + routes) * part + route_pos - stream * part
    slot_index = jnp.where(kept_mask, slot_index, -1)
    first_share = gate_num.astype(jnp.float32) / 64.0
    weights = jnp.where(kept_mask, jnp.stack([first_share, 1.0 - first_share], axis=1), 0.0)
    slot_ids = jnp.arange(expert_count * slot_count, dtype=jnp.int32)
    dispatch = jnp.any(slot_ids[:, None, None] == slot_index[None, :, :], axis=2)
    combine_hits = slot_ids[None, :, None] == slot_index[:, None, :]
    combine = jnp.sum(jnp.where(combine_hits, weights[:, None, :], 0.0), axis=2)
    return dispatch.astype(jnp.bfloat16), combine.astype(jnp.bfloat16)


def shift(value, axis, by):
    count = lax.axis_size(axis)
    return lax.ppermute(value, axis, [(i, (i + by) % count) for i in range(count)])


def add(a, b):
    return (a.astype(jnp.float32) + b.astype(jnp.float32)).astype(jnp.bfloat16)


def per_device(tokens, routes, gate_num, capacity, w_up, w_down):
    expert_count = capacity.shape[0]
    token_count, width = tokens.shape
    features = w_up.shape[0]
    slot_count = min(token_count, 3 * token_count // expert_count)
    part = slot_count // STREAMS
    count = lax.axis_size(RING)
    half = count // 2
    place = lax.axis_index(RING).astype(jnp.int32).reshape(1)
    up = w_up.T
    weights = (up, shift(up, "core", 1), w_down, shift(w_down, "core", 1))
    dispatch, combine = routing(routes, gate_num, capacity, slot_count)
    rows = jnp.dot(dispatch, tokens, preferred_element_type=jnp.float32).astype(jnp.bfloat16)
    rows = rows.reshape(STREAMS, expert_count, part, width)

    held = []
    for s in range(STREAMS):
        mine = lax.all_to_all(rows[s], "z", 0, 0, tiled=True)
        held.append({0: mine.reshape(expert_count * part, width)})
    last = (-half, half)
    for step in range(1, half + 1):
        for s in range(STREAMS):
            if step < half or last[s] < 0:
                held[s][-step] = shift(held[s][1 - step], RING, 1)
            if step < half or last[s] > 0:
                held[s][step] = shift(held[s][step - 1], RING, -1)

    own = []
    for s in range(STREAMS):
        order = [j if j in held[s] else j - count for j in range(count)]
        own.append(ffn(place, [held[s][j] for j in order], weights, features))

    ahead, behind = [None] * STREAMS, [None] * STREAMS
    for step in range(half, 0, -1):
        for s in range(STREAMS):
            if step < half or last[s] < 0:
                sent = own[s][step]
                sent = sent if ahead[s] is None else add(sent, ahead[s])
                ahead[s] = shift(sent, RING, 1)
            if step < half or last[s] > 0:
                sent = own[s][count - step]
                sent = sent if behind[s] is None else add(sent, behind[s])
                behind[s] = shift(sent, RING, -1)

    back = []
    for s in range(STREAMS):
        total = own[s][0].astype(jnp.float32) + ahead[s].astype(jnp.float32)
        total = (total + behind[s].astype(jnp.float32)).astype(jnp.bfloat16)
        total = total.reshape(expert_count, part, width)
        back.append(lax.all_to_all(total, "z", 0, 0, tiled=True).reshape(-1, width))
    length = expert_count * part
    mixed = jnp.zeros((token_count, width), jnp.float32)
    for s in range(STREAMS):
        mixed += jnp.dot(
            combine[:, s * length : (s + 1) * length],
            back[s],
            preferred_element_type=jnp.float32,
        )
    return mixed.astype(jnp.bfloat16)


def solution(mesh):
    sizes = dict(mesh.shape)
    group = sizes["expert"] // EXPERTS
    devices = mesh.devices.reshape(sizes["dp"], EXPERTS, group // 2, 2, sizes["mp"])
    fine = Mesh(devices, ("dp", "z", "yh", "core", "mp"))
    expert = ("z", "yh", "core")
    return jax.shard_map(
        per_device,
        mesh=fine,
        in_specs=(
            P(("dp", *expert), "mp"),
            P(("dp", *expert), None),
            P(("dp", *expert)),
            P(),
            P(None, (*expert, "mp")),
            P((*expert, "mp"), None),
        ),
        out_specs=P(("dp", *expert), "mp"),
        check_vma=False,
    )
```

time: 299 us -> 185 us (0.62)
  the two profiles are of different devices: /device:TPU:1 before, /device:TPU:4 now
where the time goes in v2:
time: 185 us; the launch traced here: 184 us
  starting transfers between devices  112 us (61%)
  waiting for transfers between devices  26.3 us (14%)
  blocking collectives  20.7 us (11%)
  Pallas kernels  12.1 us (7%)
  local copies, waits for them, and re-layouts  5.39 us (3%)
  other arithmetic  5.05 us (3%)
    ppermute x30, starting transfers between devices, shift(): lax.ppermute(value, axis, [(i, (i + by) % count) for i in range(count)])  100 us
    all_to_all x1, blocking collectives, per_device(): mine = lax.all_to_all(rows[s], 'z', 0, 0, tiled=True)  20.7 us
    all_to_all x2, waiting for transfers between devices, per_device(): back.append(lax.all_to_all(total, 'z', 0, 0, tiled=True).reshape(-1, width))  18.8 us
    pallas_call x2, Pallas kernels, ffn(): pl.pallas_call(ffn_body, in_specs=[pl.BlockSpec(memory_space=pltpu.SMEM)]...  12.1 us
    all_to_all x2, starting transfers between devices, per_device(): back.append(lax.all_to_all(total, 'z', 0, 0, tiled=True).reshape(-1, width))  9.06 us
    ppermute x30, waiting for transfers between devices, shift(): lax.ppermute(value, axis, [(i, (i + by) % count) for i in range(count)])  5.04 us
    unnamed x16, local copies, waits for them, and re-layouts  4.7 us
  transfers between devices with their start and end apart: 33, of which 6 were waited for; matrix products, arithmetic and copies ran while one was open for 3% of the time, Pallas kernels for 7%

profile of v2, /device:TPU:4, one launch (start us, length us, event | category | flops | bytes accessed | tf_op | source)
XLA Modules:
  0.0 184.1 jit_solution(15115156112011616539)
XLA Ops:
  0.0 2.0 %collective-permute-start.7 = (bf16[448,2048]{1,0:T(8,128)(2,1)}, bf16[448,2048]{1,0:T(8,128)(2,1)}, u32[]{:S(2)}, u32[]{:S(2)}) collective-permute-start(bf16[448,2048]{1,0:T(8,128)(2,1)} %bitcast.18), channel_id=1, source_target_pairs={{0,4},{4,0},{1,5},{5,1},{2,6},{6,2},{3,7},{7,3},{8,12},{12,8},{9,1... | collective-permute-start | bytes 5505032 | tf_op jit(solution)/shard_map/ppermute | solution.py:89
  2.1 2.4 %collective-permute-start.8 = (bf16[448,2048]{1,0:T(8,128)(2,1)}, bf16[448,2048]{1,0:T(8,128)(2,1)}, u32[]{:S(2)}, u32[]{:S(2)}) collective-permute-start(bf16[448,2048]{1,0:T(8,128)(2,1)} %refs_10_.3), channel_id=1, source_target_pairs={{0,4},{4,0},{1,5},{5,1},{2,6},{6,2},{3,7},{7,3},{8,12},{12,8},{9,1... | collective-permute-start | bytes 5505032 | tf_op jit(solution)/shard_map/ppermute | solution.py:89
  4.5 0.7 convert_reduce_fusion
  5.2 0.1 convolution_convert_fusion.1
  5.3 0.7 fusion.6
  6.0 0.8 select_reduce_fusion.1
  6.8 0.7 subtract_select_fusion
  7.5 0.2 convolution_convert_fusion
  7.8 0.7 fusion.7
  8.5 20.7 %all_to_all.20 = bf16[8,24,512]{2,1,0:T(8,128)(2,1)S(1)} all-to-all(bf16[8,24,512]{2,1,0:T(8,128)(2,1)S(1)} %bitcast.29), channel_id=1, replica_groups=mesh['dp'=4,'z'=8,'yh'=2,'core'=2,'mp'=4] {'z'}, dimensions={0} | all-to-all | bytes 393216 | tf_op jit(solution)/shard_map/all_to_all | solution.py:113
  29.2 3.4 %all-to-all-start = ((bf16[8,24,512]{2,1,0:T(8,128)(2,1)}), bf16[8,24,512]{2,1,0:T(8,128)(2,1)S(1)}, u32[]{:S(2)}, u32[]{:S(2)}) async-start(bf16[8,24,512]{2,1,0:T(8,128)(2,1)} %bitcast.3), calls=%async_computation | async-start | bytes 393216 | tf_op jit(solution)/shard_map/all_to_all | solution.py:113
  32.6 5.4 %collective-permute-start.16 = (bf16[192,512]{1,0:T(8,128)(2,1)S(1)}, bf16[192,512]{1,0:T(8,128)(2,1)S(1)}, u32[]{:S(2)}, u32[]{:S(2)}) collective-permute-start(bf16[192,512]{1,0:T(8,128)(2,1)S(1)} %bitcast.24), channel_id=1, source_target_pairs={{0,11},{1,0},{2,1},{3,2},{8,3},{9,8},{10,9},{11,10},{4,15},{5,4},{... | collective-permute-start | bytes 589832 | tf_op jit(solution)/shard_map/ppermute | solution.py:89
  38.0 1.9 %collective-permute-start.20 = (bf16[192,512]{1,0:T(8,128)(2,1)S(1)}, bf16[192,512]{1,0:T(8,128)(2,1)S(1)}, u32[]{:S(2)}, u32[]{:S(2)}) collective-permute-start(bf16[192,512]{1,0:T(8,128)(2,1)S(1)} %bitcast.25), channel_id=1, source_target_pairs={{0,1},{1,2},{2,3},{3,8},{8,9},{9,10},{10,11},{11,0},{4,5},{5,6},{6... | collective-permute-start | bytes 589832 | tf_op jit(solution)/shard_map/ppermute | solution.py:89
  39.9 2.4 %all-to-all-done = bf16[8,24,512]{2,1,0:T(8,128)(2,1)S(1)} async-done(((bf16[8,24,512]{2,1,0:T(8,128)(2,1)}), bf16[8,24,512]{2,1,0:T(8,128)(2,1)S(1)}, u32[]{:S(2)}, u32[]{:S(2)}) %all-to-all-start) | async-done | bytes 196640 | tf_op jit(solution)/shard_map/all_to_all | solution.py:113
  42.3 3.5 %collective-permute-start.3 = (bf16[192,512]{1,0:T(8,128)(2,1)S(1)}, bf16[192,512]{1,0:T(8,128)(2,1)S(1)}, u32[]{:S(2)}, u32[]{:S(2)}) collective-permute-start(bf16[192,512]{1,0:T(8,128)(2,1)S(1)} %bitcast.21), channel_id=1, source_target_pairs={{0,1},{1,2},{2,3},{3,8},{8,9},{9,10},{10,11},{11,0},{4,5},{5,6},{6... | collective-permute-start | bytes 589832 | tf_op jit(solution)/shard_map/ppermute | solution.py:89
  45.8 3.8 %collective-permute-start = (bf16[192,512]{1,0:T(8,128)(2,1)S(1)}, bf16[192,512]{1,0:T(8,128)(2,1)S(1)}, u32[]{:S(2)}, u32[]{:S(2)}) collective-permute-start(bf16[192,512]{1,0:T(8,128)(2,1)S(1)} %bitcast.22), channel_id=1, source_target_pairs={{0,11},{1,0},{2,1},{3,2},{8,3},{9,8},{10,9},{11,10},{4,15},{5,4},{... | collective-permute-start | bytes 589832 | tf_op jit(solution)/shard_map/ppermute | solution.py:89
  49.6 3.9 %collective-permute-start.17 = (bf16[192,512]{1,0:T(8,128)(2,1)S(1)}, bf16[192,512]{1,0:T(8,128)(2,1)S(1)}, u32[]{:S(2)}, u32[]{:S(2)}) collective-permute-start(bf16[192,512]{1,0:T(8,128)(2,1)S(1)} %collective-permute-done.16.refs_1_), channel_id=1, source_target_pairs={{0,11},{1,0},{2,1},{3,2},{8,3},{9,8},{10,9},{11,10},{4,15},{5,4},{... | collective-permute-start | bytes 589832 | tf_op jit(solution)/shard_map/ppermute | solution.py:89
  53.6 1.9 %collective-permute-start.21 = (bf16[192,512]{1,0:T(8,128)(2,1)S(1)}, bf16[192,512]{1,0:T(8,128)(2,1)}, u32[]{:S(2)}, u32[]{:S(2)}) collective-permute-start(bf16[192,512]{1,0:T(8,128)(2,1)S(1)} %collective-permute-done.20.refs_7_), channel_id=1, source_target_pairs={{0,1},{1,2},{2,3},{3,8},{8,9},{9,10},{10,11},{11,0},{4,5},{5,6},{6... | collective-permute-start | bytes 589832 | tf_op jit(solution)/shard_map/ppermute | solution.py:89
  55.5 2.0 %collective-permute-start.4 = (bf16[192,512]{1,0:T(8,128)(2,1)S(1)}, bf16[192,512]{1,0:T(8,128)(2,1)S(1)}, u32[]{:S(2)}, u32[]{:S(2)}) collective-permute-start(bf16[192,512]{1,0:T(8,128)(2,1)S(1)} %collective-permute-done.3.refs_7_), channel_id=1, source_target_pairs={{0,1},{1,2},{2,3},{3,8},{8,9},{9,10},{10,11},{11,0},{4,5},{5,6},{6... | collective-permute-start | bytes 589832 | tf_op jit(solution)/shard_map/ppermute | solution.py:89
  57.6 5.0 %collective-permute-start.1 = (bf16[192,512]{1,0:T(8,128)(2,1)S(1)}, bf16[192,512]{1,0:T(8,128)(2,1)}, u32[]{:S(2)}, u32[]{:S(2)}) collective-permute-start(bf16[192,512]{1,0:T(8,128)(2,1)S(1)} %collective-permute-done.refs_1_), channel_id=1, source_target_pairs={{0,11},{1,0},{2,1},{3,2},{8,3},{9,8},{10,9},{11,10},{4,15},{5,4},{... | collective-permute-start | bytes 589832 | tf_op jit(solution)/shard_map/ppermute | solution.py:89
  62.6 3.9 %collective-permute-start.18 = (bf16[192,512]{1,0:T(8,128)(2,1)S(1)}, bf16[192,512]{1,0:T(8,128)(2,1)}, u32[]{:S(2)}, u32[]{:S(2)}) collective-permute-start(bf16[192,512]{1,0:T(8,128)(2,1)S(1)} %collective-permute-done.17.refs_2_), channel_id=1, source_target_pairs={{0,11},{1,0},{2,1},{3,2},{8,3},{9,8},{10,9},{11,10},{4,15},{5,4},{... | collective-permute-start | bytes 589832 | tf_op jit(solution)/shard_map/ppermute | solution.py:89
  66.6 0.7 copy-done.4
  67.2 1.9 %collective-permute-start.22 = (bf16[192,512]{1,0:T(8,128)(2,1)}, bf16[192,512]{1,0:T(8,128)(2,1)}, u32[]{:S(2)}, u32[]{:S(2)}) collective-permute-start(bf16[192,512]{1,0:T(8,128)(2,1)} %collective-permute-done.21.refs_6_), channel_id=1, source_target_pairs={{0,1},{1,2},{2,3},{3,8},{8,9},{9,10},{10,11},{11,0},{4,5},{5,6},{6... | collective-permute-start | bytes 589832 | tf_op jit(solution)/shard_map/ppermute | solution.py:89
  69.1 1.9 %collective-permute-start.5 = (bf16[192,512]{1,0:T(8,128)(2,1)S(1)}, bf16[192,512]{1,0:T(8,128)(2,1)}, u32[]{:S(2)}, u32[]{:S(2)}) collective-permute-start(bf16[192,512]{1,0:T(8,128)(2,1)S(1)} %collective-permute-done.4.refs_6_), channel_id=1, source_target_pairs={{0,1},{1,2},{2,3},{3,8},{8,9},{9,10},{10,11},{11,0},{4,5},{5,6},{6... | collective-permute-start | bytes 589832 | tf_op jit(solution)/shard_map/ppermute | solution.py:89
  71.1 5.1 %collective-permute-start.19 = (bf16[192,512]{1,0:T(8,128)(2,1)}, bf16[192,512]{1,0:T(8,128)(2,1)S(1)}, u32[]{:S(2)}, u32[]{:S(2)}) collective-permute-start(bf16[192,512]{1,0:T(8,128)(2,1)} %collective-permute-done.18.refs_3_), channel_id=1, source_target_pairs={{0,11},{1,0},{2,1},{3,2},{8,3},{9,8},{10,9},{11,10},{4,15},{5,4},{... | collective-permute-start | bytes 589832 | tf_op jit(solution)/shard_map/ppermute | solution.py:89
  76.2 0.1 collective-permute-done.22.refs_5_
  76.3 3.9 %collective-permute-start.2 = (bf16[192,512]{1,0:T(8,128)(2,1)}, bf16[192,512]{1,0:T(8,128)(2,1)S(1)}, u32[]{:S(2)}, u32[]{:S(2)}) collective-permute-start(bf16[192,512]{1,0:T(8,128)(2,1)} %collective-permute-done.1.refs_2_), channel_id=1, source_target_pairs={{0,11},{1,0},{2,1},{3,2},{8,3},{9,8},{10,9},{11,10},{4,15},{5,4},{... | collective-permute-start | bytes 589832 | tf_op jit(solution)/shard_map/ppermute | solution.py:89
  80.2 2.0 %collective-permute-start.6 = (bf16[192,512]{1,0:T(8,128)(2,1)}, bf16[192,512]{1,0:T(8,128)(2,1)S(1)}, u32[]{:S(2)}, u32[]{:S(2)}) collective-permute-start(bf16[192,512]{1,0:T(8,128)(2,1)} %collective-permute-done.5.refs_5_), channel_id=1, source_target_pairs={{0,1},{1,2},{2,3},{3,8},{8,9},{9,10},{10,11},{11,0},{4,5},{5,6},{6... | collective-permute-start | bytes 589832 | tf_op jit(solution)/shard_map/ppermute | solution.py:89
  82.2 0.7 copy-done.6
  82.9 1.5 copy-done.2
  84.4 0.9 copy-done.5
  85.3 0.9 copy-done.7
  86.2 6.1 %ffn.3 = (bf16[192,512]{1,0:T(8,128)(2,1)S(1)}, bf16[192,512]{1,0:T(8,128)(2,1)S(1)}, bf16[192,512]{1,0:T(8,128)(2,1)S(1)}, bf16[192,512]{1,0:T(8,128)(2,1)S(1)}...) custom-call(s32[1]{0:T(128)} %bitcast.2.place_ref, ...), custom_call_target="tpu_custom_call" | custom-call | tf_op jit(solution)/shard_map/ffn/pallas_call | solution.py:49
  92.4 1.9 %collective-permute-start.23 = (bf16[192,512]{1,0:T(8,128)(2,1)S(1)}, bf16[192,512]{1,0:T(8,128)(2,1)S(1)}, u32[]{:S(2)}, u32[]{:S(2)}) collective-permute-start(bf16[192,512]{1,0:T(8,128)(2,1)S(1)} %get-tuple-element.32), channel_id=1, source_target_pairs={{0,1},{1,2},{2,3},{3,8},{8,9},{9,10},{10,11},{11,0},{4,5},{5,6},{6... | collective-permute-start | bytes 589832 | tf_op jit(solution)/shard_map/ppermute | solution.py:89
  94.3 5.1 %collective-permute-start.26 = (bf16[192,512]{1,0:T(8,128)(2,1)S(1)}, bf16[192,512]{1,0:T(8,128)(2,1)S(1)}, u32[]{:S(2)}, u32[]{:S(2)}) collective-permute-start(bf16[192,512]{1,0:T(8,128)(2,1)S(1)} %get-tuple-element.36), channel_id=1, source_target_pairs={{0,11},{1,0},{2,1},{3,2},{8,3},{9,8},{10,9},{11,10},{4,15},{5,4},{... | collective-permute-start | bytes 589832 | tf_op jit(solution)/shard_map/ppermute | solution.py:89
  99.5 6.0 %ffn.2 = (bf16[192,512]{1,0:T(8,128)(2,1)S(1)}, bf16[192,512]{1,0:T(8,128)(2,1)S(1)}, bf16[192,512]{1,0:T(8,128)(2,1)S(1)}, bf16[192,512]{1,0:T(8,128)(2,1)S(1)}...) custom-call(s32[1]{0:T(128)} %bitcast.2.place_ref, ...), custom_call_target="tpu_custom_call" | custom-call | tf_op jit(solution)/shard_map/ffn/pallas_call | solution.py:49
  105.4 1.9 %collective-permute-start.9 = (bf16[192,512]{1,0:T(8,128)(2,1)S(1)}, bf16[192,512]{1,0:T(8,128)(2,1)S(1)}, u32[]{:S(2)}, u32[]{:S(2)}) collective-permute-start(bf16[192,512]{1,0:T(8,128)(2,1)S(1)} %get-tuple-element.25), channel_id=1, source_target_pairs={{0,1},{1,2},{2,3},{3,8},{8,9},{9,10},{10,11},{11,0},{4,5},{5,6},{6... | collective-permute-start | bytes 589832 | tf_op jit(solution)/shard_map/ppermute | solution.py:89
  107.4 5.1 %collective-permute-start.13 = (bf16[192,512]{1,0:T(8,128)(2,1)S(1)}, bf16[192,512]{1,0:T(8,128)(2,1)S(1)}, u32[]{:S(2)}, u32[]{:S(2)}) collective-permute-start(bf16[192,512]{1,0:T(8,128)(2,1)S(1)} %get-tuple-element.28), channel_id=1, source_target_pairs={{0,11},{1,0},{2,1},{3,2},{8,3},{9,8},{10,9},{11,10},{4,15},{5,4},{... | collective-permute-start | bytes 589832 | tf_op jit(solution)/shard_map/ppermute | solution.py:89
  112.5 0.1 add_convert_fusion.5
  112.6 1.9 %collective-permute-start.24 = (bf16[192,512]{1,0:T(8,128)(2,1)S(1)}, bf16[192,512]{1,0:T(8,128)(2,1)S(1)}, u32[]{:S(2)}, u32[]{:S(2)}) collective-permute-start(bf16[192,512]{1,0:T(8,128)(2,1)S(1)} %add_convert_fusion.5), channel_id=1, source_target_pairs={{0,1},{1,2},{2,3},{3,8},{8,9},{9,10},{10,11},{11,0},{4,5},{5,6},{6... | collective-permute-start | bytes 589832 | tf_op jit(solution)/shard_map/ppermute | solution.py:89
  114.5 0.1 add_convert_fusion.3
  114.6 5.1 %collective-permute-start.27 = (bf16[192,512]{1,0:T(8,128)(2,1)S(1)}, bf16[192,512]{1,0:T(8,128)(2,1)S(1)}, u32[]{:S(2)}, u32[]{:S(2)}) collective-permute-start(bf16[192,512]{1,0:T(8,128)(2,1)S(1)} %add_convert_fusion.3), channel_id=1, source_target_pairs={{0,11},{1,0},{2,1},{3,2},{8,3},{9,8},{10,9},{11,10},{4,15},{5,4},{... | collective-permute-start | bytes 589832 | tf_op jit(solution)/shard_map/ppermute | solution.py:89
  119.8 1.9 %collective-permute-start.10 = (bf16[192,512]{1,0:T(8,128)(2,1)S(1)}, bf16[192,512]{1,0:T(8,128)(2,1)S(1)}, u32[]{:S(2)}, u32[]{:S(2)}) collective-permute-start(bf16[192,512]{1,0:T(8,128)(2,1)S(1)} %add_convert_fusion.11), channel_id=1, source_target_pairs={{0,1},{1,2},{2,3},{3,8},{8,9},{9,10},{10,11},{11,0},{4,5},{5,6},{6... | collective-permute-start | bytes 589832 | tf_op jit(solution)/shard_map/ppermute | solution.py:89
  121.7 0.1 add_convert_fusion.8
  121.8 5.1 %collective-permute-start.14 = (bf16[192,512]{1,0:T(8,128)(2,1)S(1)}, bf16[192,512]{1,0:T(8,128)(2,1)S(1)}, u32[]{:S(2)}, u32[]{:S(2)}) collective-permute-start(bf16[192,512]{1,0:T(8,128)(2,1)S(1)} %add_convert_fusion.8), channel_id=1, source_target_pairs={{0,11},{1,0},{2,1},{3,2},{8,3},{9,8},{10,9},{11,10},{4,15},{5,4},{... | collective-permute-start | bytes 589832 | tf_op jit(solution)/shard_map/ppermute | solution.py:89
  126.9 0.1 add_convert_fusion.4
  127.0 1.9 %collective-permute-start.25 = (bf16[192,512]{1,0:T(8,128)(2,1)S(1)}, bf16[192,512]{1,0:T(8,128)(2,1)S(1)}, u32[]{:S(2)}, u32[]{:S(2)}) collective-permute-start(bf16[192,512]{1,0:T(8,128)(2,1)S(1)} %add_convert_fusion.4), channel_id=1, source_target_pairs={{0,1},{1,2},{2,3},{3,8},{8,9},{9,10},{10,11},{11,0},{4,5},{5,6},{6... | collective-permute-start | bytes 589832 | tf_op jit(solution)/shard_map/ppermute | solution.py:89
  129.0 5.1 %collective-permute-start.28 = (bf16[192,512]{1,0:T(8,128)(2,1)S(1)}, bf16[192,512]{1,0:T(8,128)(2,1)S(1)}, u32[]{:S(2)}, u32[]{:S(2)}) collective-permute-start(bf16[192,512]{1,0:T(8,128)(2,1)S(1)} %add_convert_fusion.2), channel_id=1, source_target_pairs={{0,11},{1,0},{2,1},{3,2},{8,3},{9,8},{10,9},{11,10},{4,15},{5,4},{... | collective-permute-start | bytes 589832 | tf_op jit(solution)/shard_map/ppermute | solution.py:89
  134.2 1.9 %collective-permute-start.11 = (bf16[192,512]{1,0:T(8,128)(2,1)S(1)}, bf16[192,512]{1,0:T(8,128)(2,1)S(1)}, u32[]{:S(2)}, u32[]{:S(2)}) collective-permute-start(bf16[192,512]{1,0:T(8,128)(2,1)S(1)} %add_convert_fusion.10), channel_id=1, source_target_pairs={{0,1},{1,2},{2,3},{3,8},{8,9},{9,10},{10,11},{11,0},{4,5},{5,6},{6... | collective-permute-start | bytes 589832 | tf_op jit(solution)/shard_map/ppermute | solution.py:89
  136.1 0.1 add_convert_fusion.7
  136.2 5.1 %collective-permute-start.15 = (bf16[192,512]{1,0:T(8,128)(2,1)S(1)}, bf16[192,512]{1,0:T(8,128)(2,1)S(1)}, u32[]{:S(2)}, u32[]{:S(2)}) collective-permute-start(bf16[192,512]{1,0:T(8,128)(2,1)S(1)} %add_convert_fusion.7), channel_id=1, source_target_pairs={{0,11},{1,0},{2,1},{3,2},{8,3},{9,8},{10,9},{11,10},{4,15},{5,4},{... | collective-permute-start | bytes 589832 | tf_op jit(solution)/shard_map/ppermute | solution.py:89
  141.3 3.3 %collective-permute-done.11 = bf16[192,512]{1,0:T(8,128)(2,1)S(1)} collective-permute-done((bf16[192,512]{1,0:T(8,128)(2,1)S(1)}, bf16[192,512]{1,0:T(8,128)(2,1)S(1)}, u32[]{:S(2)}, u32[]{:S(2)}) %collective-permute-start.11) | collective-permute-done | bytes 196640 | tf_op jit(solution)/shard_map/ppermute | solution.py:89
  144.7 1.9 %collective-permute-start.12 = (bf16[192,512]{1,0:T(8,128)(2,1)S(1)}, bf16[192,512]{1,0:T(8,128)(2,1)S(1)}, u32[]{:S(2)}, u32[]{:S(2)}) collective-permute-start(bf16[192,512]{1,0:T(8,128)(2,1)S(1)} %add_convert_fusion.9), channel_id=1, source_target_pairs={{0,1},{1,2},{2,3},{3,8},{8,9},{9,10},{10,11},{11,0},{4,5},{5,6},{6... | collective-permute-start | bytes 589832 | tf_op jit(solution)/shard_map/ppermute | solution.py:89
  146.7 5.1 %collective-permute-start.29 = (bf16[192,512]{1,0:T(8,128)(2,1)S(1)}, bf16[192,512]{1,0:T(8,128)(2,1)S(1)}, u32[]{:S(2)}, u32[]{:S(2)}) collective-permute-start(bf16[192,512]{1,0:T(8,128)(2,1)S(1)} %add_convert_fusion.1), channel_id=1, source_target_pairs={{0,11},{1,0},{2,1},{3,2},{8,3},{9,8},{10,9},{11,10},{4,15},{5,4},{... | collective-permute-start | bytes 589832 | tf_op jit(solution)/shard_map/ppermute | solution.py:89
  151.8 1.6 collective-permute-done.12
  153.4 0.7 add_convert_fusion.6
  154.2 5.7 %all-to-all-start.1 = ((bf16[8,24,512]{2,1,0:T(8,128)(2,1)}), bf16[8,24,512]{2,1,0:T(8,128)(2,1)S(1)}, u32[]{:S(2)}, u32[]{:S(2)}) async-start(bf16[8,24,512]{2,1,0:T(8,128)(2,1)} %bitcast.6), calls=%async_computation.1 | async-start | bytes 393216 | tf_op jit(solution)/shard_map/all_to_all | solution.py:145
  159.9 0.7 add_convert_fusion
  160.6 9.5 %all-to-all-done.1 = bf16[8,24,512]{2,1,0:T(8,128)(2,1)S(1)} async-done(((bf16[8,24,512]{2,1,0:T(8,128)(2,1)}), bf16[8,24,512]{2,1,0:T(8,128)(2,1)S(1)}, u32[]{:S(2)}, u32[]{:S(2)}) %all-to-all-start.1) | async-done | bytes 196640 | tf_op jit(solution)/shard_map/all_to_all | solution.py:145
  170.1 3.4 %all-to-all-start.3 = ((bf16[8,24,512]{2,1,0:T(8,128)(2,1)}), bf16[8,24,512]{2,1,0:T(8,128)(2,1)S(1)}, u32[]{:S(2)}, u32[]{:S(2)}) async-start(bf16[8,24,512]{2,1,0:T(8,128)(2,1)} %bitcast.10), calls=%async_computation.3 | async-start | bytes 393216 | tf_op jit(solution)/shard_map/all_to_all | solution.py:145
  173.5 0.1 select_reduce_fusion
  173.6 0.2 fusion.3
  173.8 9.4 %all-to-all-done.3 = bf16[8,24,512]{2,1,0:T(8,128)(2,1)S(1)} async-done(((bf16[8,24,512]{2,1,0:T(8,128)(2,1)}), bf16[8,24,512]{2,1,0:T(8,128)(2,1)S(1)}, u32[]{:S(2)}, u32[]{:S(2)}) %all-to-all-start.3) | async-done | bytes 196640 | tf_op jit(solution)/shard_map/all_to_all | solution.py:145
  183.2 0.9 fusion
  (45 shorter events, 0.4 us)
Async XLA Ops:
  0.0 7.5 %copy-start = (bf16[128,512]{1,0:T(8,128)(2,1)S(1)}, bf16[128,512]{1,0:T(8,128)(2,1)}, u32[]{:S(2)}) copy-start(bf16[128,512]{1,0:T(8,128)(2,1)} %param.6) | copy-start | bytes 393220
  0.0 82.9 %copy-start.1 = (bf16[2048,448]{0,1:T(8,128)(2,1)S(1)}, bf16[2048,448]{0,1:T(8,128)(2,1)}, u32[]{:S(2)}) copy-start(bf16[2048,448]{0,1:T(8,128)(2,1)} %param.10) | copy-start | bytes 5505028
  0.0 82.8 %collective-permute-start.7 = (bf16[448,2048]{1,0:T(8,128)(2,1)}, bf16[448,2048]{1,0:T(8,128)(2,1)}, u32[]{:S(2)}, u32[]{:S(2)}) collective-permute-start(bf16[448,2048]{1,0:T(8,128)(2,1)} %bitcast.18), channel_id=1, source_target_pairs={{0,4},{4,0},{1,5},{5,1},{2,6},{6,2},{3,7},{7,3},{8,12},{12,8},{9,1... | collective-permute-start | bytes 5505032 | tf_op jit(solution)/shard_map/ppermute | solution.py:89
  2.1 80.8 %collective-permute-start.8 = (bf16[448,2048]{1,0:T(8,128)(2,1)}, bf16[448,2048]{1,0:T(8,128)(2,1)}, u32[]{:S(2)}, u32[]{:S(2)}) collective-permute-start(bf16[448,2048]{1,0:T(8,128)(2,1)} %refs_10_.3), channel_id=1, source_target_pairs={{0,4},{4,0},{1,5},{5,1},{2,6},{6,2},{3,7},{7,3},{8,12},{12,8},{9,1... | collective-permute-start | bytes 5505032 | tf_op jit(solution)/shard_map/ppermute | solution.py:89
  29.2 13.1 %all-to-all-start = ((bf16[8,24,512]{2,1,0:T(8,128)(2,1)}), bf16[8,24,512]{2,1,0:T(8,128)(2,1)S(1)}, u32[]{:S(2)}, u32[]{:S(2)}) async-start(bf16[8,24,512]{2,1,0:T(8,128)(2,1)} %bitcast.3), calls=%async_computation | async-start | bytes 393216 | tf_op jit(solution)/shard_map/all_to_all | solution.py:113
  32.6 13.2 %collective-permute-start.16 = (bf16[192,512]{1,0:T(8,128)(2,1)S(1)}, bf16[192,512]{1,0:T(8,128)(2,1)S(1)}, u32[]{:S(2)}, u32[]{:S(2)}) collective-permute-start(bf16[192,512]{1,0:T(8,128)(2,1)S(1)} %bitcast.24), channel_id=1, source_target_pairs={{0,11},{1,0},{2,1},{3,2},{8,3},{9,8},{10,9},{11,10},{4,15},{5,4},{... | collective-permute-start | bytes 589832 | tf_op jit(solution)/shard_map/ppermute | solution.py:89
  38.0 11.6 %collective-permute-start.20 = (bf16[192,512]{1,0:T(8,128)(2,1)S(1)}, bf16[192,512]{1,0:T(8,128)(2,1)S(1)}, u32[]{:S(2)}, u32[]{:S(2)}) collective-permute-start(bf16[192,512]{1,0:T(8,128)(2,1)S(1)} %bitcast.25), channel_id=1, source_target_pairs={{0,1},{1,2},{2,3},{3,8},{8,9},{9,10},{10,11},{11,0},{4,5},{5,6},{6... | collective-permute-start | bytes 589832 | tf_op jit(solution)/shard_map/ppermute | solution.py:89
  42.3 11.3 %collective-permute-start.3 = (bf16[192,512]{1,0:T(8,128)(2,1)S(1)}, bf16[192,512]{1,0:T(8,128)(2,1)S(1)}, u32[]{:S(2)}, u32[]{:S(2)}) collective-permute-start(bf16[192,512]{1,0:T(8,128)(2,1)S(1)} %bitcast.21), channel_id=1, source_target_pairs={{0,1},{1,2},{2,3},{3,8},{8,9},{9,10},{10,11},{11,0},{4,5},{5,6},{6... | collective-permute-start | bytes 589832 | tf_op jit(solution)/shard_map/ppermute | solution.py:89
  45.8 9.7 %collective-permute-start = (bf16[192,512]{1,0:T(8,128)(2,1)S(1)}, bf16[192,512]{1,0:T(8,128)(2,1)S(1)}, u32[]{:S(2)}, u32[]{:S(2)}) collective-permute-start(bf16[192,512]{1,0:T(8,128)(2,1)S(1)} %bitcast.22), channel_id=1, source_target_pairs={{0,11},{1,0},{2,1},{3,2},{8,3},{9,8},{10,9},{11,10},{4,15},{5,4},{... | collective-permute-start | bytes 589832 | tf_op jit(solution)/shard_map/ppermute | solution.py:89
  49.6 7.9 %collective-permute-start.17 = (bf16[192,512]{1,0:T(8,128)(2,1)S(1)}, bf16[192,512]{1,0:T(8,128)(2,1)S(1)}, u32[]{:S(2)}, u32[]{:S(2)}) collective-permute-start(bf16[192,512]{1,0:T(8,128)(2,1)S(1)} %collective-permute-done.16.refs_1_), channel_id=1, source_target_pairs={{0,11},{1,0},{2,1},{3,2},{8,3},{9,8},{10,9},{11,10},{4,15},{5,4},{... | collective-permute-start | bytes 589832 | tf_op jit(solution)/shard_map/ppermute | solution.py:89
  53.6 9.0 %collective-permute-start.21 = (bf16[192,512]{1,0:T(8,128)(2,1)S(1)}, bf16[192,512]{1,0:T(8,128)(2,1)}, u32[]{:S(2)}, u32[]{:S(2)}) collective-permute-start(bf16[192,512]{1,0:T(8,128)(2,1)S(1)} %collective-permute-done.20.refs_7_), channel_id=1, source_target_pairs={{0,1},{1,2},{2,3},{3,8},{8,9},{9,10},{10,11},{11,0},{4,5},{5,6},{6... | collective-permute-start | bytes 589832 | tf_op jit(solution)/shard_map/ppermute | solution.py:89
  55.5 11.7 %collective-permute-start.4 = (bf16[192,512]{1,0:T(8,128)(2,1)S(1)}, bf16[192,512]{1,0:T(8,128)(2,1)S(1)}, u32[]{:S(2)}, u32[]{:S(2)}) collective-permute-start(bf16[192,512]{1,0:T(8,128)(2,1)S(1)} %collective-permute-done.3.refs_7_), channel_id=1, source_target_pairs={{0,1},{1,2},{2,3},{3,8},{8,9},{9,10},{10,11},{11,0},{4,5},{5,6},{6... | collective-permute-start | bytes 589832 | tf_op jit(solution)/shard_map/ppermute | solution.py:89
  57.6 11.6 %collective-permute-start.1 = (bf16[192,512]{1,0:T(8,128)(2,1)S(1)}, bf16[192,512]{1,0:T(8,128)(2,1)}, u32[]{:S(2)}, u32[]{:S(2)}) collective-permute-start(bf16[192,512]{1,0:T(8,128)(2,1)S(1)} %collective-permute-done.refs_1_), channel_id=1, source_target_pairs={{0,11},{1,0},{2,1},{3,2},{8,3},{9,8},{10,9},{11,10},{4,15},{5,4},{... | collective-permute-start | bytes 589832 | tf_op jit(solution)/shard_map/ppermute | solution.py:89
  62.6 8.5 %collective-permute-start.18 = (bf16[192,512]{1,0:T(8,128)(2,1)S(1)}, bf16[192,512]{1,0:T(8,128)(2,1)}, u32[]{:S(2)}, u32[]{:S(2)}) collective-permute-start(bf16[192,512]{1,0:T(8,128)(2,1)S(1)} %collective-permute-done.17.refs_2_), channel_id=1, source_target_pairs={{0,11},{1,0},{2,1},{3,2},{8,3},{9,8},{10,9},{11,10},{4,15},{5,4},{... | collective-permute-start | bytes 589832 | tf_op jit(solution)/shard_map/ppermute | solution.py:89
  66.5 0.7 copy-start.4
  67.2 9.1 %collective-permute-start.22 = (bf16[192,512]{1,0:T(8,128)(2,1)}, bf16[192,512]{1,0:T(8,128)(2,1)}, u32[]{:S(2)}, u32[]{:S(2)}) collective-permute-start(bf16[192,512]{1,0:T(8,128)(2,1)} %collective-permute-done.21.refs_6_), channel_id=1, source_target_pairs={{0,1},{1,2},{2,3},{3,8},{8,9},{9,10},{10,11},{11,0},{4,5},{5,6},{6... | collective-permute-start | bytes 589832 | tf_op jit(solution)/shard_map/ppermute | solution.py:89
  69.1 11.0 %collective-permute-start.5 = (bf16[192,512]{1,0:T(8,128)(2,1)S(1)}, bf16[192,512]{1,0:T(8,128)(2,1)}, u32[]{:S(2)}, u32[]{:S(2)}) collective-permute-start(bf16[192,512]{1,0:T(8,128)(2,1)S(1)} %collective-permute-done.4.refs_6_), channel_id=1, source_target_pairs={{0,1},{1,2},{2,3},{3,8},{8,9},{9,10},{10,11},{11,0},{4,5},{5,6},{6... | collective-permute-start | bytes 589832 | tf_op jit(solution)/shard_map/ppermute | solution.py:89
  71.1 11.1 %collective-permute-start.19 = (bf16[192,512]{1,0:T(8,128)(2,1)}, bf16[192,512]{1,0:T(8,128)(2,1)S(1)}, u32[]{:S(2)}, u32[]{:S(2)}) collective-permute-start(bf16[192,512]{1,0:T(8,128)(2,1)} %collective-permute-done.18.refs_3_), channel_id=1, source_target_pairs={{0,11},{1,0},{2,1},{3,2},{8,3},{9,8},{10,9},{11,10},{4,15},{5,4},{... | collective-permute-start | bytes 589832 | tf_op jit(solution)/shard_map/ppermute | solution.py:89
  76.3 23.1 %collective-permute-start.2 = (bf16[192,512]{1,0:T(8,128)(2,1)}, bf16[192,512]{1,0:T(8,128)(2,1)S(1)}, u32[]{:S(2)}, u32[]{:S(2)}) collective-permute-start(bf16[192,512]{1,0:T(8,128)(2,1)} %collective-permute-done.1.refs_2_), channel_id=1, source_target_pairs={{0,11},{1,0},{2,1},{3,2},{8,3},{9,8},{10,9},{11,10},{4,15},{5,4},{... | collective-permute-start | bytes 589832 | tf_op jit(solution)/shard_map/ppermute | solution.py:89
  80.2 19.3 %collective-permute-start.6 = (bf16[192,512]{1,0:T(8,128)(2,1)}, bf16[192,512]{1,0:T(8,128)(2,1)S(1)}, u32[]{:S(2)}, u32[]{:S(2)}) collective-permute-start(bf16[192,512]{1,0:T(8,128)(2,1)} %collective-permute-done.5.refs_5_), channel_id=1, source_target_pairs={{0,1},{1,2},{2,3},{3,8},{8,9},{9,10},{10,11},{11,0},{4,5},{5,6},{6... | collective-permute-start | bytes 589832 | tf_op jit(solution)/shard_map/ppermute | solution.py:89
  82.2 0.7 copy-start.6
  82.9 1.5 copy-start.2
  84.4 0.9 copy-start.5
  85.3 0.9 copy-start.7
  86.2 13.2 %copy-start.3 = (bf16[448,2048]{1,0:T(8,128)(2,1)S(1)}, bf16[448,2048]{1,0:T(8,128)(2,1)}, u32[]{:S(2)}) copy-start(bf16[448,2048]{1,0:T(8,128)(2,1)} %refs_10_.3) | copy-start | bytes 5505028
  92.4 20.2 %collective-permute-start.23 = (bf16[192,512]{1,0:T(8,128)(2,1)S(1)}, bf16[192,512]{1,0:T(8,128)(2,1)S(1)}, u32[]{:S(2)}, u32[]{:S(2)}) collective-permute-start(bf16[192,512]{1,0:T(8,128)(2,1)S(1)} %get-tuple-element.32), channel_id=1, source_target_pairs={{0,1},{1,2},{2,3},{3,8},{8,9},{9,10},{10,11},{11,0},{4,5},{5,6},{6... | collective-permute-start | bytes 589832 | tf_op jit(solution)/shard_map/ppermute | solution.py:89
  94.3 20.2 %collective-permute-start.26 = (bf16[192,512]{1,0:T(8,128)(2,1)S(1)}, bf16[192,512]{1,0:T(8,128)(2,1)S(1)}, u32[]{:S(2)}, u32[]{:S(2)}) collective-permute-start(bf16[192,512]{1,0:T(8,128)(2,1)S(1)} %get-tuple-element.36), channel_id=1, source_target_pairs={{0,11},{1,0},{2,1},{3,2},{8,3},{9,8},{10,9},{11,10},{4,15},{5,4},{... | collective-permute-start | bytes 589832 | tf_op jit(solution)/shard_map/ppermute | solution.py:89
  105.4 14.3 %collective-permute-start.9 = (bf16[192,512]{1,0:T(8,128)(2,1)S(1)}, bf16[192,512]{1,0:T(8,128)(2,1)S(1)}, u32[]{:S(2)}, u32[]{:S(2)}) collective-permute-start(bf16[192,512]{1,0:T(8,128)(2,1)S(1)} %get-tuple-element.25), channel_id=1, source_target_pairs={{0,1},{1,2},{2,3},{3,8},{8,9},{9,10},{10,11},{11,0},{4,5},{5,6},{6... | collective-permute-start | bytes 589832 | tf_op jit(solution)/shard_map/ppermute | solution.py:89
  107.4 14.3 %collective-permute-start.13 = (bf16[192,512]{1,0:T(8,128)(2,1)S(1)}, bf16[192,512]{1,0:T(8,128)(2,1)S(1)}, u32[]{:S(2)}, u32[]{:S(2)}) collective-permute-start(bf16[192,512]{1,0:T(8,128)(2,1)S(1)} %get-tuple-element.28), channel_id=1, source_target_pairs={{0,11},{1,0},{2,1},{3,2},{8,3},{9,8},{10,9},{11,10},{4,15},{5,4},{... | collective-permute-start | bytes 589832 | tf_op jit(solution)/shard_map/ppermute | solution.py:89
  112.6 14.3 %collective-permute-start.24 = (bf16[192,512]{1,0:T(8,128)(2,1)S(1)}, bf16[192,512]{1,0:T(8,128)(2,1)S(1)}, u32[]{:S(2)}, u32[]{:S(2)}) collective-permute-start(bf16[192,512]{1,0:T(8,128)(2,1)S(1)} %add_convert_fusion.5), channel_id=1, source_target_pairs={{0,1},{1,2},{2,3},{3,8},{8,9},{9,10},{10,11},{11,0},{4,5},{5,6},{6... | collective-permute-start | bytes 589832 | tf_op jit(solution)/shard_map/ppermute | solution.py:89
  114.6 14.3 %collective-permute-start.27 = (bf16[192,512]{1,0:T(8,128)(2,1)S(1)}, bf16[192,512]{1,0:T(8,128)(2,1)S(1)}, u32[]{:S(2)}, u32[]{:S(2)}) collective-permute-start(bf16[192,512]{1,0:T(8,128)(2,1)S(1)} %add_convert_fusion.3), channel_id=1, source_target_pairs={{0,11},{1,0},{2,1},{3,2},{8,3},{9,8},{10,9},{11,10},{4,15},{5,4},{... | collective-permute-start | bytes 589832 | tf_op jit(solution)/shard_map/ppermute | solution.py:89
  119.8 14.3 %collective-permute-start.10 = (bf16[192,512]{1,0:T(8,128)(2,1)S(1)}, bf16[192,512]{1,0:T(8,128)(2,1)S(1)}, u32[]{:S(2)}, u32[]{:S(2)}) collective-permute-start(bf16[192,512]{1,0:T(8,128)(2,1)S(1)} %add_convert_fusion.11), channel_id=1, source_target_pairs={{0,1},{1,2},{2,3},{3,8},{8,9},{9,10},{10,11},{11,0},{4,5},{5,6},{6... | collective-permute-start | bytes 589832 | tf_op jit(solution)/shard_map/ppermute | solution.py:89
  121.8 14.3 %collective-permute-start.14 = (bf16[192,512]{1,0:T(8,128)(2,1)S(1)}, bf16[192,512]{1,0:T(8,128)(2,1)S(1)}, u32[]{:S(2)}, u32[]{:S(2)}) collective-permute-start(bf16[192,512]{1,0:T(8,128)(2,1)S(1)} %add_convert_fusion.8), channel_id=1, source_target_pairs={{0,11},{1,0},{2,1},{3,2},{8,3},{9,8},{10,9},{11,10},{4,15},{5,4},{... | collective-permute-start | bytes 589832 | tf_op jit(solution)/shard_map/ppermute | solution.py:89
  127.0 32.9 %collective-permute-start.25 = (bf16[192,512]{1,0:T(8,128)(2,1)S(1)}, bf16[192,512]{1,0:T(8,128)(2,1)S(1)}, u32[]{:S(2)}, u32[]{:S(2)}) collective-permute-start(bf16[192,512]{1,0:T(8,128)(2,1)S(1)} %add_convert_fusion.4), channel_id=1, source_target_pairs={{0,1},{1,2},{2,3},{3,8},{8,9},{9,10},{10,11},{11,0},{4,5},{5,6},{6... | collective-permute-start | bytes 589832 | tf_op jit(solution)/shard_map/ppermute | solution.py:89
  129.0 17.6 %collective-permute-start.28 = (bf16[192,512]{1,0:T(8,128)(2,1)S(1)}, bf16[192,512]{1,0:T(8,128)(2,1)S(1)}, u32[]{:S(2)}, u32[]{:S(2)}) collective-permute-start(bf16[192,512]{1,0:T(8,128)(2,1)S(1)} %add_convert_fusion.2), channel_id=1, source_target_pairs={{0,11},{1,0},{2,1},{3,2},{8,3},{9,8},{10,9},{11,10},{4,15},{5,4},{... | collective-permute-start | bytes 589832 | tf_op jit(solution)/shard_map/ppermute | solution.py:89
  134.2 10.4 %collective-permute-start.11 = (bf16[192,512]{1,0:T(8,128)(2,1)S(1)}, bf16[192,512]{1,0:T(8,128)(2,1)S(1)}, u32[]{:S(2)}, u32[]{:S(2)}) collective-permute-start(bf16[192,512]{1,0:T(8,128)(2,1)S(1)} %add_convert_fusion.10), channel_id=1, source_target_pairs={{0,1},{1,2},{2,3},{3,8},{8,9},{9,10},{10,11},{11,0},{4,5},{5,6},{6... | collective-permute-start | bytes 589832 | tf_op jit(solution)/shard_map/ppermute | solution.py:89
  136.2 15.6 %collective-permute-start.15 = (bf16[192,512]{1,0:T(8,128)(2,1)S(1)}, bf16[192,512]{1,0:T(8,128)(2,1)S(1)}, u32[]{:S(2)}, u32[]{:S(2)}) collective-permute-start(bf16[192,512]{1,0:T(8,128)(2,1)S(1)} %add_convert_fusion.7), channel_id=1, source_target_pairs={{0,11},{1,0},{2,1},{3,2},{8,3},{9,8},{10,9},{11,10},{4,15},{5,4},{... | collective-permute-start | bytes 589832 | tf_op jit(solution)/shard_map/ppermute | solution.py:89
  144.7 8.8 %collective-permute-start.12 = (bf16[192,512]{1,0:T(8,128)(2,1)S(1)}, bf16[192,512]{1,0:T(8,128)(2,1)S(1)}, u32[]{:S(2)}, u32[]{:S(2)}) collective-permute-start(bf16[192,512]{1,0:T(8,128)(2,1)S(1)} %add_convert_fusion.9), channel_id=1, source_target_pairs={{0,1},{1,2},{2,3},{3,8},{8,9},{9,10},{10,11},{11,0},{4,5},{5,6},{6... | collective-permute-start | bytes 589832 | tf_op jit(solution)/shard_map/ppermute | solution.py:89
  146.7 13.2 %collective-permute-start.29 = (bf16[192,512]{1,0:T(8,128)(2,1)S(1)}, bf16[192,512]{1,0:T(8,128)(2,1)S(1)}, u32[]{:S(2)}, u32[]{:S(2)}) collective-permute-start(bf16[192,512]{1,0:T(8,128)(2,1)S(1)} %add_convert_fusion.1), channel_id=1, source_target_pairs={{0,11},{1,0},{2,1},{3,2},{8,3},{9,8},{10,9},{11,10},{4,15},{5,4},{... | collective-permute-start | bytes 589832 | tf_op jit(solution)/shard_map/ppermute | solution.py:89
  154.2 15.9 %all-to-all-start.1 = ((bf16[8,24,512]{2,1,0:T(8,128)(2,1)}), bf16[8,24,512]{2,1,0:T(8,128)(2,1)S(1)}, u32[]{:S(2)}, u32[]{:S(2)}) async-start(bf16[8,24,512]{2,1,0:T(8,128)(2,1)} %bitcast.6), calls=%async_computation.1 | async-start | bytes 393216 | tf_op jit(solution)/shard_map/all_to_all | solution.py:145
  170.1 13.1 %all-to-all-start.3 = ((bf16[8,24,512]{2,1,0:T(8,128)(2,1)}), bf16[8,24,512]{2,1,0:T(8,128)(2,1)S(1)}, u32[]{:S(2)}, u32[]{:S(2)}) async-start(bf16[8,24,512]{2,1,0:T(8,128)(2,1)} %bitcast.10), calls=%async_computation.3 | async-start | bytes 393216 | tf_op jit(solution)/shard_map/all_to_all | solution.py:145
